TPU v7x, 32 devices: a whole 2x2x4 slice. The times are simulated.
32 devices in a mesh: replica: 8 (over y, x, core), mp: 4 (over z).
Axes of the slice: x: 2, y: 2, z: 4, core: 2. Of those that a mesh axis runs over, the one named last changes fastest.
Arguments:
- pseudo_grad: bfloat16 [8, 2, 3072, 2048], P('replica', None, None, 'mp'), may hold values from -6 to 6
- outer_params: float32 [2, 3072, 2048], P(None, 'replica', 'mp'), may hold values from -6 to 6
- momentum: float32 [2, 3072, 2048], P(None, 'replica', 'mp'), may hold values from -3 to 3
- acts: bfloat16 [1024, 3072], P('replica', 'mp'), may hold values from -6 to 6
- queries: bfloat16 [1024, 2048], P('replica', 'mp'), may hold values from -6 to 6
- keys: bfloat16 [1024, 2048], P('replica', 'mp'), may hold values from -6 to 6
- doc_ids: int32 [1024], P('replica'), may hold values from 0 to 31, never falling along the last dimension, each value on 1 to 64 neighbouring positions
Outputs:
- new_outer: float32 [2, 3072, 2048], P(None, 'replica', 'mp')
- new_momentum: float32 [2, 3072, 2048], P(None, 'replica', 'mp')
- new_local: bfloat16 [8, 3072, 2048], P('replica', None, 'mp')
Inputs may be any that keep to these rules, and one draw needn't show every extreme that they name: doc_ids never fall along the rows; each document covers 1 to 64 positions.
All inputs are finite; a program needn't handle non-finite values.
Results may differ from a plain program's by a relative error of at most 0.0037.
The roundings to bfloat16 on the way count: a program that leaves them out, or rounds other values in their place, can miss the bound.
Values may be sent and summed in bfloat16 or wider, within the bound.
A program may use at most 64 MiB of HBM per device.

v0:
```python
import jax
import jax.numpy as jnp
from jax import lax
from jax.sharding import PartitionSpec as P

HD = 256
norm_eps = 1e-06
outer_rate = 0.7
outer_beta = 0.9
inner_rate = 0.1


def attend(query, key_rows, value_rows, doc_rows):
    count = query.shape[0]
    scores = jnp.einsum(
        "qhd,khd->hqk", query, key_rows, preferred_element_type=jnp.float32
    ) * query.shape[2] ** (-0.5)
    row_pos = lax.broadcasted_iota(jnp.int32, (count, count), 0)
    col_pos = lax.broadcasted_iota(jnp.int32, (count, count), 1)
    allowed = (row_pos >= col_pos) & (doc_rows[:, None] == doc_rows[None, :])
    scores = jnp.where(allowed[None], scores, -1e30)
    probs = jax.nn.softmax(scores, axis=-1).astype(jnp.bfloat16)
    context = jnp.einsum("hqk,khd->qhd", probs, value_rows, preferred_element_type=jnp.float32)
    return context.astype(jnp.bfloat16)


def outer_update(summed, params_rows, moment_rows, workers):
    delta = summed / workers
    moment_next = outer_beta * moment_rows + delta
    params_next = params_rows - outer_rate * (delta + outer_beta * moment_next)
    return (params_next, moment_next)


def shards(pseudo_grad, outer_params, momentum, acts, queries, keys, doc_ids):
    workers = lax.axis_size("replica")
    groups = lax.axis_size("mp")
    full_x = lax.all_gather(acts, "mp", axis=1, tiled=True)
    blocks = lax.all_to_all(pseudo_grad, "replica", split_axis=2, concat_axis=0, tiled=True)
    summed = jnp.sum(blocks.astype(jnp.float32), axis=0)
    new_outer, new_momentum = outer_update(summed, outer_params, momentum, workers)
    weights = lax.all_gather(new_outer.astype(jnp.bfloat16), "replica", axis=1, tiled=True)
    count, width = full_x.shape
    cols = weights.shape[2]
    heads_here = cols // HD
    all_cols = cols * groups
    rows_f = full_x.astype(jnp.float32)
    normed = (
        rows_f * lax.rsqrt(jnp.mean(rows_f * rows_f, axis=-1, keepdims=True) + norm_eps)
    ).astype(jnp.bfloat16)
    values = (
        jnp.dot(normed, weights[0], preferred_element_type=jnp.float32) * width ** (-0.5)
    ).astype(jnp.bfloat16)
    query = queries.reshape(count, heads_here, HD)
    keyed = keys.reshape(count, heads_here, HD)

    def attn_fn(c):
        return attend(query, keyed, c, doc_ids)

    context, pullback = jax.vjp(attn_fn, values.reshape(count, heads_here, HD))
    ctx = context.reshape(count, cols)
    partial_branch = lax.dot_general(
        ctx, weights[1], (((1,), (1,)), ((), ())), preferred_element_type=jnp.float32
    ) * all_cols ** (-0.5)
    branch = lax.psum(partial_branch.astype(jnp.bfloat16), "mp").astype(jnp.float32)
    dout = (rows_f + branch - jnp.roll(rows_f, -1, axis=0)).astype(jnp.bfloat16)
    dctx = (
        jnp.dot(dout, weights[1], preferred_element_type=jnp.float32) * all_cols ** (-0.5)
    ).astype(jnp.bfloat16)
    pulled = pullback(dctx.reshape(count, heads_here, HD))[0]
    grad = lax.dot_general(
        normed,
        pulled.reshape(count, cols),
        (((0,), (0,)), ((), ())),
        preferred_element_type=jnp.float32,
    ) * width ** (-0.5)
    squares = lax.psum(jnp.sum(grad * grad), "mp")
    rms = jnp.sqrt(squares / (width * all_cols) + norm_eps)
    new_local = (weights[0].astype(jnp.float32) - inner_rate * grad / rms).astype(jnp.bfloat16)
    return (new_outer, new_momentum, new_local[None])


def solution(mesh):
    placed = (
        P("replica", None, None, "mp"),
        P(None, "replica", "mp"),
        P(None, "replica", "mp"),
        P("replica", "mp"),
        P("replica", "mp"),
        P("replica", "mp"),
        P("replica"),
    )
    return jax.shard_map(
        shards,
        mesh=mesh,
        in_specs=placed,
        out_specs=(P(None, "replica", "mp"), P(None, "replica", "mp"), P("replica", None, "mp")),
        check_vma=False,
    )
```

profile of v0, /device:TPU:0, one launch (start us, length us, event | category | flops | bytes accessed | tf_op | source)
XLA Modules:
  0.0 232.5 jit_solution(10670747100160510871)
XLA Ops:
  7.2 0.0 all-gather.2.cloned.1.call-start
  7.2 11.1 %copy.23 = bf16[1,2,3072,512]{3,1,0,2:T(2,128)(2,1)S(1)} copy(bf16[1,2,3072,512]{3,2,1,0:T(8,128)(2,1)} %param.7) | data formatting | bytes 12582912 | tf_op args[0]
  18.3 76.5 %all_to_all.4 = bf16[1,2,3072,512]{3,1,0,2:T(2,128)(2,1)S(1)} all-to-all(bf16[1,2,3072,512]{3,1,0,2:T(2,128)(2,1)S(1)} %copy.23), channel_id=1, replica_groups=mesh['replica'=8,'mp'=4] {'replica'}, dimensions={2} | all-to-all | bytes 12582912 | tf_op jit(solution)/shard_map/all_to_all | solution.py:38
  94.8 0.0 copy-start
  94.8 0.0 copy-start.1
  94.8 6.3 %convert_reduce_fusion = f32[2,384,512]{2,0,1:T(2,128)S(1)} fusion(bf16[2,8,384,512]{3,0,2,1:T(2,128)(2,1)S(1)} %bitcast.46), kind=kLoop, calls=%fused_computation.1 | loop fusion | flops 5898240 | bytes 7864320 | tf_op jit(solution)/shard_map/reduce_sum | solution.py:39
  101.1 0.0 copy-done
  101.1 0.0 copy-done.1
  101.1 0.0 copy-start.3
  101.1 0.0 copy-start.4
  101.1 0.0 copy-start.5
  101.1 0.0 copy-start.2
  101.1 2.7 %fusion.21 = (bf16[2,384,512]{2,1,0:T(8,128)(2,1)}, f32[2,384,512]{2,1,0:T(8,128)}, f32[2,384,512]{2,1,0:T(8,128)}) fusion(f32[2,384,512]{2,1,0:T(8,128)S(1)} %copy-done, f32[2,384,512]{2,0,1:T(2,128)S(1)} %convert_reduce_fusion, f32[2,384,512]{2,1,0:T(8,128)S(1)} %copy-done.1), kind=kLoop, calls=%fused_computation.38 | loop fusion | flops 3145728 | bytes 8650752 | tf_op jit(solution)/shard_map/convert_element_type | solution.py:41
  103.8 0.0 all-gather.2.cloned.1.call-update
  103.8 0.0 all-reduce.2.cloned.1.call-start
  103.9 0.0 copy-done.3
  103.9 0.1 fusion.19
  104.0 0.0 copy-done.4
  104.0 0.0 copy-done.5
  104.0 0.2 fusion.12
  104.2 0.1 fusion.22
  104.3 0.0 copy-done.2
  104.3 19.8 %all_gather.7 = bf16[128,3072]{1,0:T(8,128)(2,1)S(1)} all-gather(bf16[128,768]{1,0:T(8,128)(2,1)S(1)} %copy-done.2), channel_id=1, replica_groups=mesh['replica'=8,'mp'=4] {'mp'}, dimensions={1}, use_global_device_ids=true | all-gather | bytes 983040 | tf_op jit(solution)/shard_map/all_gather | solution.py:37
  124.1 0.2 multiply_reduce_fusion.1
  124.3 24.4 %all-gather.2.cloned.1.call-done = bf16[2,3072,512]{2,1,0:T(8,128)(2,1)} async-done(((bf16[2,384,512]{2,1,0:T(8,128)(2,1)}), bf16[2,3072,512]{2,1,0:T(8,128)(2,1)}) %all-gather.2.cloned.1.call-update) | async-done | bytes 6291472 | tf_op jit(solution)/shard_map/all_gather | solution.py:41
  148.7 2.5 %fusion.9 = bf16[128,512]{1,0:T(8,128)(2,1)S(1)} fusion(bf16[2,3072,512]{2,1,0:T(8,128)(2,1)} %all-gather.2.cloned.1.call-done, bf16[128,3072]{1,0:T(8,128)(2,1)S(1)} %all_gather.7, f32[128]{0:T(128)S(1)} %add_rsqrt_fusion), kind=kOutput, calls=%fused_computation.23 | convolution fusion | flops 403963904 | bytes 4063744 | tf_op jit(solution)/shard_map/dot_general | solution.py:51
  151.3 0.1 copy.33
  151.4 0.2 convolution_convert_fusion.1
  151.6 3.9 %fusion.1 = bf16[128,3072]{1,0:T(8,128)(2,1)} fusion(bf16[128,512]{0,1:T(8,128)(2,1)S(1)} %bitcast.52, bf16[2,3072,512]{2,1,0:T(8,128)(2,1)} %all-gather.2.cloned.1.call-done), kind=kOutput, calls=%fused_computation.5 | convolution fusion | flops 403439616 | bytes 4063232 | tf_op jit(solution)/shard_map/dot_general | solution.py:61
  155.5 0.0 all-reduce.2.cloned.1.call-update
  155.6 0.2 slice.22
  155.8 43.8 %all-reduce.2.cloned.1.call-done = bf16[128,3072]{1,0:T(8,128)(2,1)} async-done(((bf16[128,3072]{1,0:T(8,128)(2,1)}), bf16[128,3072]{1,0:T(8,128)(2,1)}) %all-reduce.2.cloned.1.call-update) | async-done | bytes 786448 | tf_op jit(solution)/shard_map/psum | solution.py:64
  199.6 2.8 %fusion.10 = bf16[128,512]{1,0:T(8,128)(2,1)S(1)} fusion(bf16[2,3072,512]{2,1,0:T(8,128)(2,1)} %all-gather.2.cloned.1.call-done, f32[1,3072]{1,0:T(1,128)S(1)} %slice.23, f32[127,3072]{1,0:T(8,128)S(1)} %slice.22, bf16[128,3072]{1,0:T(8,128)(2,1)} %all-reduce.2.cloned.1.call-done, bf16[128,3072]{1,0:T(8,128)(2,1)S(1)} %all_gather.7), kind=kOutput, calls=%fused_computation.24 | convolution fusion | flops 405143552 | bytes 6422528 | tf_op jit(solution)/shard_map/dot_general | solution.py:67
  202.4 0.1 copy.34
  202.5 0.2 convolution_convert_fusion
  202.7 5.1 %multiply_reduce_fusion = (f32[]{:T(128)}, f32[3072,512]{1,0:T(8,128)}) fusion(bf16[128,512]{0,1:T(8,128)(2,1)S(1)} %bitcast.47, bf16[128,3072]{1,0:T(8,128)(2,1)S(1)} %all_gather.7, f32[128]{0:T(128)S(1)} %add_rsqrt_fusion), kind=kOutput, calls=%fused_computation.3 | convolution fusion | flops 408551424 | bytes 7209476 | tf_op jit(solution)/shard_map/dot_general | solution.py:70
  207.8 10.6 %psum.15 = f32[]{:T(128)} all-reduce(f32[]{:T(128)} %get-tuple-element.6), channel_id=1, replica_groups=mesh['replica'=8,'mp'=4] {'mp'}, use_global_device_ids=true, to_apply=%region_6.7 | all-reduce | flops 1 | bytes 8 | tf_op jit(solution)/shard_map/psum | solution.py:76
  219.1 6.5 %fusion.2 = bf16[1,3072,512]{2,1,0:T(8,128)(2,1)} fusion(f32[]{:T(128)S(6)} %sqrt.3, f32[3072,512]{1,0:T(8,128)} %get-tuple-element.7, bf16[2,3072,512]{2,1,0:T(8,128)(2,1)} %all-gather.2.cloned.1.call-done), kind=kLoop, calls=%fused_computation.8 | loop fusion | flops 7864320 | bytes 12582916 | tf_op jit(solution)/shard_map/broadcast_in_dim | solution.py:79
  (2 shorter events, 0.0 us)
Async XLA Ops:
  7.2 141.6 %all-gather.2.cloned.1.call-start = ((), (), s32[]{:S(2)}) async-start(), calls=%async_computation.1 | async-start | bytes 7077888 | tf_op jit(solution)/shard_map/all_gather | solution.py:41
  94.8 6.3 %copy-start = (f32[2,384,512]{2,1,0:T(8,128)S(1)}, f32[2,384,512]{2,1,0:T(8,128)}, u32[]{:S(2)}) copy-start(f32[2,384,512]{2,1,0:T(8,128)} %param.8) | copy-start | bytes 4718596
  94.8 6.3 %copy-start.1 = (f32[2,384,512]{2,1,0:T(8,128)S(1)}, f32[2,384,512]{2,1,0:T(8,128)}, u32[]{:S(2)}) copy-start(f32[2,384,512]{2,1,0:T(8,128)} %param.9) | copy-start | bytes 4718596
  101.1 2.8 %copy-start.3 = (s32[128]{0:T(128)S(1)}, s32[128]{0:T(128)}, u32[]{:S(2)}) copy-start(s32[128]{0:T(128)} %param.13) | copy-start | bytes 1540
  101.1 2.9 %copy-start.4 = (bf16[128,512]{1,0:T(8,128)(2,1)S(1)}, bf16[128,512]{1,0:T(8,128)(2,1)}, u32[]{:S(2)}) copy-start(bf16[128,512]{1,0:T(8,128)(2,1)} %param.12) | copy-start | bytes 393220
  101.1 2.9 %copy-start.5 = (bf16[128,512]{1,0:T(8,128)(2,1)S(1)}, bf16[128,512]{1,0:T(8,128)(2,1)}, u32[]{:S(2)}) copy-start(bf16[128,512]{1,0:T(8,128)(2,1)} %param.11) | copy-start | bytes 393220
  101.1 3.1 %copy-start.2 = (bf16[128,768]{1,0:T(8,128)(2,1)S(1)}, bf16[128,768]{1,0:T(8,128)(2,1)}, u32[]{:S(2)}) copy-start(bf16[128,768]{1,0:T(8,128)(2,1)} %param.10) | copy-start | bytes 589828
  103.8 95.7 %all-reduce.2.cloned.1.call-start = ((), (), s32[]{:S(2)}) async-start(), calls=%async_computation.2 | async-start | bytes 1572864 | tf_op jit(solution)/shard_map/psum | solution.py:64
Sparse Core Ops, SparseCore 0:
  103.9 44.7 all-gather.1
  155.7 43.8 all-reduce.1
where the time goes:
time: 233 us; the launch traced here: 232 us
  blocking collectives  107 us (46%)
  waiting for transfers between devices  68.2 us (29%)
  other arithmetic  15.8 us (7%)
  matrix products  15 us (6%)
  between operations  14.9 us (6%)
  local copies, waits for them, and re-layouts  11.6 us (5%)
    all_to_all x1, blocking collectives, shards(): lax.all_to_all(pseudo_grad, 'replica', split_axis=2, concat_axis=0, tiled...  76.5 us
    psum x1, waiting for transfers between devices, shards(): lax.psum(partial_branch.astype(jnp.bfloat16), 'mp').astype(jnp.float32)  43.8 us
    all_gather x1, waiting for transfers between devices, shards(): lax.all_gather(new_outer.astype(jnp.bfloat16), 'replica', axis=1, tiled=T...  24.4 us
    all_gather x1, blocking collectives, shards(): full_x = lax.all_gather(acts, 'mp', axis=1, tiled=True)  19.8 us
    unnamed x13, local copies, waits for them, and re-layouts  11.1 us
    psum x1, blocking collectives, shards(): squares = lax.psum(jnp.sum(grad * grad), 'mp')  10.6 us
    broadcast_in_dim x1, other arithmetic, shards(): return (new_outer, new_momentum, new_local[None])  6.48 us
    reduce_sum x1, other arithmetic, shards(): summed = jnp.sum(blocks.astype(jnp.float32), axis=0)  6.26 us
  transfers between devices with their start and end apart: 2, of which 2 were waited for; matrix products, arithmetic and copies ran while one was open for 0% of the time, Pallas kernels for 0%

commit v1 on v0

--- a/solution.py
+++ b/solution.py
@@ -34,7 +34,7 @@
 def shards(pseudo_grad, outer_params, momentum, acts, queries, keys, doc_ids):
     workers = lax.axis_size("replica")
     groups = lax.axis_size("mp")
-    full_x = lax.all_gather(acts, "mp", axis=1, tiled=True)
+    full_x = jnp.concatenate(lax.all_gather(acts, "mp"), axis=1)
     blocks = lax.all_to_all(pseudo_grad, "replica", split_axis=2, concat_axis=0, tiled=True)
     summed = jnp.sum(blocks.astype(jnp.float32), axis=0)
     new_outer, new_momentum = outer_update(summed, outer_params, momentum, workers)

time: 233 us -> 234 us (level)
  local copies, waits for them, and re-layouts: 11.6 us -> 20.9 us
  waiting for transfers between devices: 68.2 us -> 59.1 us
    psum x1, waiting for transfers between devices: 43.8 us -> 35.6 us  [shards(): lax.psum(partial_branch.astype(jnp.bfloat16), 'mp').astype(jnp.float32)]
    convert_element_type x0 -> x3, local copies, waits for them, and re-layouts: none -> 5.21 us  [the longest x2 4.84 us: shards(): rows_f = full_x.astype(jnp.float32)]
    slice x2 -> x4, local copies, waits for them, and re-layouts: 0.21 us -> 3.44 us  [shards(): dout = (rows_f + branch - jnp.roll(rows_f, -1, axis=0)).astype(jnp.bfloat16)]
    unnamed x13 -> x21, local copies, waits for them, and re-layouts: 11.1 us -> 12 us
  transfers between devices with their start and end apart: 2 -> 2, of which waited for: 2 -> 2; matrix products, arithmetic and copies ran while one was open for 0% -> 4% of each run, Pallas kernels for 0% -> 0%
where the time goes in v1:
time: 234 us
  blocking collectives  107 us (46%)
  waiting for transfers between devices  59.1 us (25%)
  local copies, waits for them, and re-layouts  20.9 us (9%)
  other arithmetic  16.2 us (7%)
  matrix products  15.2 us (6%)
  between operations  14.9 us (6%)
    all_to_all x1, blocking collectives, shards(): lax.all_to_all(pseudo_grad, 'replica', split_axis=2, concat_axis=0, tiled...  76.5 us
    psum x1, waiting for transfers between devices, shards(): lax.psum(partial_branch.astype(jnp.bfloat16), 'mp').astype(jnp.float32)  35.6 us
    all_gather x1, waiting for transfers between devices, shards(): lax.all_gather(new_outer.astype(jnp.bfloat16), 'replica', axis=1, tiled=T...  23.5 us
    all_gather x1, blocking collectives, shards(): full_x = jnp.concatenate(lax.all_gather(acts, 'mp'), axis=1)  19.8 us
    unnamed x21, local copies, waits for them, and re-layouts  12 us
    psum x1, blocking collectives, shards(): squares = lax.psum(jnp.sum(grad * grad), 'mp')  10.6 us
    broadcast_in_dim x1, other arithmetic, shards(): return (new_outer, new_momentum, new_local[None])  6.48 us
    reduce_sum x1, other arithmetic, shards(): summed = jnp.sum(blocks.astype(jnp.float32), axis=0)  6.26 us
  transfers between devices with their start and end apart: 2, of which 2 were waited for; matrix products, arithmetic and copies ran while one was open for 4% of the time, Pallas kernels for 0%

profile of v1, /device:TPU:0, one launch (start us, length us, event | category | flops | bytes accessed | tf_op | source)
XLA Modules:
  0.0 233.5 jit_solution(5605690547960112061)
XLA Ops:
  7.2 0.0 all-gather.3.cloned.1.call-start
  7.2 11.1 %copy.46 = bf16[1,2,3072,512]{3,1,0,2:T(2,128)(2,1)S(1)} copy(bf16[1,2,3072,512]{3,2,1,0:T(8,128)(2,1)} %param.7) | data formatting | bytes 12582912 | tf_op args[0]
  18.3 76.5 %all_to_all.4 = bf16[1,2,3072,512]{3,1,0,2:T(2,128)(2,1)S(1)} all-to-all(bf16[1,2,3072,512]{3,1,0,2:T(2,128)(2,1)S(1)} %copy.46), channel_id=1, replica_groups=mesh['replica'=8,'mp'=4] {'replica'}, dimensions={2} | all-to-all | bytes 12582912 | tf_op jit(solution)/shard_map/all_to_all | solution.py:38
  94.8 0.0 copy-start.4
  94.8 0.0 copy-start.5
  94.8 6.3 %convert_reduce_fusion = f32[2,384,512]{2,0,1:T(2,128)S(1)} fusion(bf16[2,8,384,512]{3,0,2,1:T(2,128)(2,1)S(1)} %bitcast.60), kind=kLoop, calls=%fused_computation.1 | loop fusion | flops 5898240 | bytes 7864320 | tf_op jit(solution)/shard_map/reduce_sum | solution.py:39
  101.1 0.0 copy-done.4
  101.1 0.0 copy-done.5
  101.1 0.0 copy-start.6
  101.1 2.7 %fusion.23 = (bf16[2,384,512]{2,1,0:T(8,128)(2,1)}, f32[2,384,512]{2,1,0:T(8,128)}, f32[2,384,512]{2,1,0:T(8,128)}) fusion(f32[2,384,512]{2,1,0:T(8,128)S(1)} %copy-done.4, f32[2,384,512]{2,0,1:T(2,128)S(1)} %convert_reduce_fusion, f32[2,384,512]{2,1,0:T(8,128)S(1)} %copy-done.5), kind=kLoop, calls=%fused_computation.41 | loop fusion | flops 3145728 | bytes 8650752 | tf_op jit(solution)/shard_map/convert_element_type | solution.py:41
  103.8 0.0 all-gather.3.cloned.1.call-update
  103.8 0.0 all-reduce.2.cloned.1.call-start
  103.8 0.0 copy-done.6
  103.9 19.8 %all-gather = bf16[512,768]{1,0:T(8,128)(2,1)S(1)} all-gather(bf16[128,768]{1,0:T(8,128)(2,1)S(1)} %copy-done.6), channel_id=2, replica_groups=mesh['replica'=8,'mp'=4] {'mp'}, dimensions={0}, use_global_device_ids=true | all-gather | bytes 983040 | tf_op jit(solution)/shard_map/all_gather | solution.py:37
  123.7 0.2 fusion.5
  123.9 0.0 copy-start.7
  123.9 0.0 copy-start.8
  124.0 0.0 copy-start.9
  124.0 0.3 fusion.16
  124.3 0.4 copy.48
  124.7 0.0 copy-done.7
  124.7 0.0 copy-start.2
  124.7 0.1 fusion.21
  124.8 0.1 copy-done.8
  124.9 0.1 copy-done.9
  124.9 0.2 fusion.14
  125.1 0.1 fusion.24
  125.2 23.5 %all-gather.3.cloned.1.call-done = bf16[2,3072,512]{2,1,0:T(8,128)(2,1)} async-done(((bf16[2,384,512]{2,1,0:T(8,128)(2,1)}), bf16[2,3072,512]{2,1,0:T(8,128)(2,1)}) %all-gather.3.cloned.1.call-update) | async-done | bytes 6291472 | tf_op jit(solution)/shard_map/all_gather | solution.py:41
  148.7 2.5 %fusion.11 = bf16[128,512]{1,0:T(8,128)(2,1)S(1)} fusion(bf16[128,3072]{0,1:T(8,128)(2,1)S(1)} %bitcast.64, bf16[2,3072,512]{2,1,0:T(8,128)(2,1)} %all-gather.3.cloned.1.call-done), kind=kOutput, calls=%fused_computation.26 | convolution fusion | flops 402784256 | bytes 4063232 | tf_op jit(solution)/shard_map/dot_general | solution.py:51
  151.2 0.0 copy-done.2
  151.2 0.1 copy.61
  151.3 0.2 convolution_convert_fusion.1
  151.6 4.0 %fusion.1 = bf16[128,3072]{1,0:T(8,128)(2,1)} fusion(bf16[128,512]{0,1:T(8,128)(2,1)S(1)} %bitcast.72, bf16[2,3072,512]{2,1,0:T(8,128)(2,1)} %all-gather.3.cloned.1.call-done), kind=kOutput, calls=%fused_computation.5 | convolution fusion | flops 403439616 | bytes 4063232 | tf_op jit(solution)/shard_map/dot_general | solution.py:61
  155.5 0.0 all-reduce.2.cloned.1.call-update
  155.5 0.1 convert_bitcast_fusion
  155.7 1.3 slice.30
  157.0 1.7 copy.49
  158.7 0.0 copy-start
  158.7 3.1 %copy.54 = f32[128,3072]{1,0:T(8,128)} copy(f32[128,3072]{0,1:T(8,128)} %bitcast.62) | data formatting | bytes 3145728 | tf_op jit(solution)/shard_map/convert_element_type | solution.py:46
  161.8 0.0 copy-done
  161.8 0.5 copy.55
  162.3 0.0 copy-start.1
  162.3 1.7 copy.56
  164.0 35.6 %all-reduce.2.cloned.1.call-done = bf16[128,3072]{1,0:T(8,128)(2,1)} async-done(((bf16[128,3072]{1,0:T(8,128)(2,1)}), bf16[128,3072]{1,0:T(8,128)(2,1)}) %all-reduce.2.cloned.1.call-update) | async-done | bytes 786448 | tf_op jit(solution)/shard_map/psum | solution.py:64
  199.6 0.0 copy-done.1
  199.6 3.2 %fusion.12 = bf16[128,512]{1,0:T(8,128)(2,1)S(1)} fusion(bf16[2,3072,512]{2,1,0:T(8,128)(2,1)} %all-gather.3.cloned.1.call-done, f32[1,3072]{1,0:T(1,128)S(1)} %bitcast.69, f32[127,3072]{1,0:T(8,128)} %copy.56, f32[128,3072]{1,0:T(8,128)S(1)} %copy-done.1, bf16[128,3072]{1,0:T(8,128)(2,1)} %all-reduce.2.cloned.1.call-done), kind=kOutput, calls=%fused_computation.27 | convolution fusion | flops 404750336 | bytes 7221248 | tf_op jit(solution)/shard_map/dot_general | solution.py:67
  202.8 0.0 copy-start.3
  202.8 0.1 copy.62
  202.9 0.2 convolution_convert_fusion
  203.2 0.8 copy-done.3
  203.9 5.0 %multiply_reduce_fusion = (f32[]{:T(128)}, f32[3072,512]{1,0:T(8,128)}) fusion(bf16[128,3072]{0,1:T(8,128)(2,1)S(1)} %bitcast.65, bf16[128,512]{0,1:T(8,128)(2,1)S(1)} %bitcast.66), kind=kOutput, calls=%fused_computation.3 | convolution fusion | flops 407371776 | bytes 7208964 | tf_op jit(solution)/shard_map/dot_general | solution.py:70
  208.9 10.6 %psum.15 = f32[]{:T(128)} all-reduce(f32[]{:T(128)} %get-tuple-element.6), channel_id=1, replica_groups=mesh['replica'=8,'mp'=4] {'mp'}, use_global_device_ids=true, to_apply=%region_6.7 | all-reduce | flops 1 | bytes 8 | tf_op jit(solution)/shard_map/psum | solution.py:76
  220.2 6.5 %fusion.2 = bf16[1,3072,512]{2,1,0:T(8,128)(2,1)} fusion(f32[]{:T(128)S(6)} %sqrt.3, f32[3072,512]{1,0:T(8,128)} %get-tuple-element.7, bf16[2,3072,512]{2,1,0:T(8,128)(2,1)} %all-gather.3.cloned.1.call-done), kind=kLoop, calls=%fused_computation.8 | loop fusion | flops 7864320 | bytes 12582916 | tf_op jit(solution)/shard_map/broadcast_in_dim | solution.py:79
  (2 shorter events, 0.0 us)
Async XLA Ops:
  7.2 141.5 %all-gather.3.cloned.1.call-start = ((), (), s32[]{:S(2)}) async-start(), calls=%async_computation.1 | async-start | bytes 7077888 | tf_op jit(solution)/shard_map/all_gather | solution.py:41
  94.8 6.3 %copy-start.4 = (f32[2,384,512]{2,1,0:T(8,128)S(1)}, f32[2,384,512]{2,1,0:T(8,128)}, u32[]{:S(2)}) copy-start(f32[2,384,512]{2,1,0:T(8,128)} %param.8) | copy-start | bytes 4718596
  94.8 6.3 %copy-start.5 = (f32[2,384,512]{2,1,0:T(8,128)S(1)}, f32[2,384,512]{2,1,0:T(8,128)}, u32[]{:S(2)}) copy-start(f32[2,384,512]{2,1,0:T(8,128)} %param.9) | copy-start | bytes 4718596
  101.1 2.8 %copy-start.6 = (bf16[128,768]{1,0:T(8,128)(2,1)S(1)}, bf16[128,768]{1,0:T(8,128)(2,1)}, u32[]{:S(2)}) copy-start(bf16[128,768]{1,0:T(8,128)(2,1)} %param.10) | copy-start | bytes 589828
  103.8 95.8 %all-reduce.2.cloned.1.call-start = ((), (), s32[]{:S(2)}) async-start(), calls=%async_computation.2 | async-start | bytes 1572864 | tf_op jit(solution)/shard_map/psum | solution.py:64
  123.9 0.7 copy-start.7
  123.9 0.9 copy-start.8
  124.0 1.0 copy-start.9
  124.7 26.5 %copy-start.2 = (bf16[128,4,768]{0,2,1:T(8,128)(2,1)}, bf16[128,4,768]{0,2,1:T(8,128)(2,1)S(1)}, u32[]{:S(2)}) copy-start(bf16[128,4,768]{0,2,1:T(8,128)(2,1)S(1)} %copy.48) | copy-start | bytes 2359300
  158.7 3.1 %copy-start = (f32[127,4,768]{2,0,1:T(8,128)S(1)}, f32[127,4,768]{2,0,1:T(8,128)}, u32[]{:S(2)}) copy-start(f32[127,4,768]{2,0,1:T(8,128)} %slice.30) | copy-start | bytes 4681732
  162.3 37.2 %copy-start.1 = (f32[128,3072]{1,0:T(8,128)S(1)}, f32[128,3072]{1,0:T(8,128)}, u32[]{:S(2)}) copy-start(f32[128,3072]{1,0:T(8,128)} %copy.54) | copy-start | bytes 4718596
  202.8 1.1 copy-start.3
Sparse Core Ops, SparseCore 0:
  103.9 44.7 all-gather.2
  155.7 43.8 all-reduce.1
